TPU v7x, 32 devices: a whole 2x2x4 slice. The times are simulated.
32 devices in a mesh: group: 4 (over y, x), dom: 8 (over z, core).
Axes of the slice: x: 2, y: 2, z: 4, core: 2. Of those that a mesh axis runs over, the one named last changes fastest.
Arguments:
- p_start: float32 [1024, 128], P(('group', 'dom')), may hold values from -60 to 60
- r_start: float32 [1024, 128], P(('group', 'dom')), may hold values from -60 to 60
- diag_shift: float32 [1024, 128], P(('group', 'dom')), may hold values from 0.5 to 2
- shifts: float32 [8], replicated, may hold values from 0.5 to 1.5
- block_values: float32 [1024, 6, 128, 128], P(('group', 'dom')), may hold values from -0.21875 to 0.21875
- block_cols: int32 [1024, 6], P(('group', 'dom')), may hold values from 0 to 95, as said below
- live_slots: int32 [1024], P(('group', 'dom')), may hold values from 2 to 6, as said below
- needed: int32 [32, 4, 16], P(('group', 'dom')), may hold values from 0 to 31
Outputs:
- basis: float32 [17, 1024, 128], P(None, ('group', 'dom'))
- gram: float32 [17, 17], replicated
Inputs may be any that keep to these rules, and one draw needn't show every extreme that they name: `block_cols`: slot 0 of block row b is the row itself (b mod 32); a value below 32 names a block row of the same device, a value 32 + k * 16 + h names entry h of the device's list k of needed. Devices with dom index 0 never use list 0 in used slots, devices with the last dom index never list 1. Slots from live_slots on hold values in range but are not used. `live_slots`: the first block row of every device uses all 6 slots. needed[d, k] lists the local block rows that device d reads from its source s_k(d), in the order of its extended field.
All inputs are finite; a program needn't handle non-finite values.
Results may differ from a plain program's by a relative error of at most 0.0001.
Values sent between devices are 32-bit elements; how exact they have to be, the bound alone decides.
A program may use at most 64 MiB of HBM per device.

v0:
```python
import functools

import jax
import jax.numpy as jnp
from jax import lax
from jax.experimental import pallas as pl
from jax.experimental.pallas import tpu as pltpu
from jax.sharding import PartitionSpec as P

MESH = pl.DeviceIdType.MESH
SUB = 8
PACK = 16
CHUNK_ROWS = 4


def split(x):
    hi = x.astype(jnp.bfloat16)
    lo = (x - hi.astype(jnp.float32)).astype(jnp.bfloat16)
    return hi, lo


def kernel(n_group, n_dom, shifts, cols, live, needed, p0, r0, diag, a_hbm, basis, gram,
           a_v, xp0, xp1, xr0, xr1, f_v, spread, idx, fields, g_own, g_all,
           a_sem, send_sem, recv_sem, g_send, g_recv):
    rows, slots, bs, _ = a_v.shape
    depth = shifts.shape[0]
    halo = needed.shape[1]
    chunks = a_sem.shape[0]
    per = rows // chunks
    tiles = bs // SUB
    zero_row = 5 * rows
    n = n_group * n_dom
    g, m = lax.axis_index("group"), lax.axis_index("dom")
    me = g * n_dom + m
    xs = ((xp0, xp1), (xr0, xr1))

    def chunk(c):
        part = pl.ds(c * per, per)
        return pltpu.make_async_copy(a_hbm.at[part], a_v.at[part], a_sem.at[c])

    for c in range(chunks):
        chunk(c).start()

    for field in xs:
        for ref in field:
            ref[pl.ds(rows, 2 * rows), :] = jnp.zeros((2 * rows, bs), jnp.float32)
            ref[pl.ds(zero_row, SUB), :] = jnp.zeros((SUB, bs), jnp.float32)
    xp0[pl.ds(0, rows), :] = p0[...]
    xr0[pl.ds(0, rows), :] = r0[...]

    barrier = pltpu.get_barrier_semaphore()

    def greet(d, carry):
        to = lax.rem(me + d, n)
        pl.semaphore_signal(barrier, inc=1, device_id=(to // n_dom, lax.rem(to, n_dom)), device_id_type=MESH)
        return carry

    lax.fori_loop(1, n, greet, 0)
    pl.semaphore_wait(barrier, n - 1)

    peers = (
        (g, lax.rem(m + 1, n_dom)),
        (g, lax.rem(m + n_dom - 1, n_dom)),
        (lax.rem(g + 1, n_group), m),
        (lax.rem(g + n_group - 1, n_group), m),
    )

    def copy(which, par, k):
        ref = xs[which][par]
        return pltpu.make_async_remote_copy(
            src_ref=ref.at[pl.ds(0, rows)],
            dst_ref=ref.at[pl.ds((1 + k) * rows, rows)],
            send_sem=send_sem.at[which, par, k],
            recv_sem=recv_sem.at[which, par, k],
            device_id=peers[k],
            device_id_type=MESH,
        )

    def guarded(ok, fn):
        if ok is None:
            fn()
        else:
            pl.when(ok)(fn)

    sends = (m < n_dom - 1, m > 0, None, None)
    recvs = (m > 0, m < n_dom - 1, None, None)
    order = (2, 3, 0, 1)

    def start(which, par):
        for k in order:
            guarded(sends[k], lambda k=k: copy(which, par, k).start())

    def wait_send(which, par):
        for k in order:
            guarded(sends[k], lambda k=k: copy(which, par, k).wait_send())

    def wait_recv(which, par):
        for k in order:
            guarded(recvs[k], lambda k=k: copy(which, par, k).wait_recv())

    start(0, 0)
    start(1, 0)

    def place(b, carry):
        for s in range(slots):
            c = cols[b, s]
            e = jnp.maximum(c - rows, 0)
            k = e // halo
            far = (1 + k) * rows + needed[k, lax.rem(e, halo)]
            at = jnp.where(c < rows, c, far)
            idx[b * slots + s] = jnp.where(s < live[b], at, zero_row)
        return carry

    lax.fori_loop(0, rows, place, 0)

    fields[...] = jnp.zeros_like(fields)
    basis[0] = p0[...]
    basis[depth + 1] = r0[...]
    fields[:, 0, :] = p0[...]
    fields[:, depth + 1, :] = r0[...]

    units = bs // PACK
    l_id = lax.broadcasted_iota(jnp.int32, spread.shape, 0)
    c_id = lax.broadcasted_iota(jnp.int32, spread.shape, 1)
    spread[...] = jnp.where((l_id // bs) % units == c_id // PACK, 1.0, 0.0).astype(jnp.bfloat16)
    z_row = lax.broadcasted_iota(jnp.int32, (rows * PACK, bs), 0)
    z_col = lax.broadcasted_iota(jnp.int32, (rows * PACK, bs), 1)
    z_keep = z_row % PACK == z_col % PACK

    def rows_of(which, par, lo, hi):
        x = xs[which][par]

        def body(b, carry):
            acc = [None] * tiles
            for s in range(slots):
                xv = jnp.broadcast_to(x[pl.ds(idx[b * slots + s], 1), :], (SUB, bs))
                for t in range(tiles):
                    term = a_v[b, s, pl.ds(t * SUB, SUB), :] * xv
                    acc[t] = term if s == 0 else acc[t] + term
            at = pl.ds(pl.multiple_of(b * PACK, PACK), PACK)
            for u in range(units):
                high, low = split(jnp.concatenate([acc[2 * u], acc[2 * u + 1]], axis=0))
                f_v[which, at, pl.ds(u * bs, bs)] = high
                f_v[which, at, pl.ds((units + u) * bs, bs)] = low
            return carry

        lax.fori_loop(lo, hi, body, 0)

    def finish(which, par, step):
        z = jnp.dot(f_v[which], spread[...], preferred_element_type=jnp.float32)
        y = jnp.where(z_keep, z, 0.0).reshape(rows, PACK, bs).sum(axis=1)
        return y + (diag[...] - shifts[step - 1]) * xs[which][par][pl.ds(0, rows), :]

    def emit(which, step, y):
        column = step if which == 0 else depth + 1 + step
        last = depth if which == 0 else depth - 1
        if step < last:
            xs[which][step % 2][pl.ds(0, rows), :] = y
            start(which, step % 2)
        basis[column] = y
        fields[:, column, :] = y

    for step in range(1, depth + 1):
        par = (step - 1) % 2
        chains = (0, 1) if step < depth else (0,)
        if step == 1:
            wait_recv(0, par)
            wait_recv(1, par)
            for c in range(chunks):
                chunk(c).wait()
                for which in chains:
                    rows_of(which, par, c * per, (c + 1) * per)
        for which in chains:
            if step > 1:
                wait_recv(which, par)
                rows_of(which, par, 0, rows)
            y = finish(which, par, step)
            if step > 1:
                wait_send(which, 1 - par)
            emit(which, step, y)
    wait_send(0, (depth - 1) % 2)
    wait_send(1, (depth - 2) % 2)

    def gram_row(b, acc):
        hi, lo = split(fields[b])
        both = jnp.concatenate([hi, lo], axis=0)
        return acc + lax.dot_general(
            both, both, (((1,), (1,)), ((), ())), preferred_element_type=jnp.float32
        )

    width = fields.shape[1]
    acc = lax.fori_loop(0, rows, gram_row, jnp.zeros((2 * width, 2 * width), jnp.float32))
    top = acc[:width] + acc[width:]
    part = top[:, :width] + top[:, width:]
    g_own[...] = jnp.concatenate([part, jnp.zeros((width, bs - width), jnp.float32)], axis=1)

    def share(d):
        to = lax.rem(me + d, n)
        return pltpu.make_async_remote_copy(
            src_ref=g_own,
            dst_ref=g_all.at[me],
            send_sem=g_send.at[d],
            recv_sem=g_recv.at[me],
            device_id=(to // n_dom, lax.rem(to, n_dom)),
            device_id_type=MESH,
        )

    def arrival(source):
        return pltpu.make_async_remote_copy(
            src_ref=g_own,
            dst_ref=g_all.at[source],
            send_sem=g_send.at[0],
            recv_sem=g_recv.at[source],
            device_id=(source // n_dom, lax.rem(source, n_dom)),
            device_id_type=MESH,
        )

    def send_one(d, carry):
        share(d).start()
        return carry

    def take_one(d, carry):
        arrival(lax.rem(me + d, n)).wait_recv()
        return carry

    def sent_one(d, carry):
        share(d).wait_send()
        return carry

    lax.fori_loop(1, n, send_one, 0)
    g_all[me] = g_own[...]
    lax.fori_loop(1, n, take_one, 0)
    lax.fori_loop(1, n, sent_one, 0)
    total = lax.fori_loop(1, n, lambda i, t: t + g_all[i], g_all[0])
    count = basis.shape[0]
    gram[...] = total[:count, :count] * (1.0 / (n * rows * bs))


def per_device(n_group, n_dom, p_start, r_start, diag_shift, shifts, block_values, block_cols, live_slots, needed):
    rows, bs = p_start.shape
    slots = block_values.shape[1]
    depth = shifts.shape[0]
    columns = 2 * depth + 1
    width = -(-columns // 16) * 16
    n = n_group * n_dom
    chunks = rows // CHUNK_ROWS
    smem = pl.BlockSpec(memory_space=pltpu.SMEM)
    vmem = pl.BlockSpec(memory_space=pltpu.VMEM)
    ext = pltpu.VMEM((5 * rows + SUB, bs), jnp.float32)
    return pl.pallas_call(
        functools.partial(kernel, n_group, n_dom),
        out_shape=(
            jax.ShapeDtypeStruct((columns, rows, bs), jnp.float32),
            jax.ShapeDtypeStruct((columns, columns), jnp.float32),
        ),
        in_specs=[smem, smem, smem, smem, vmem, vmem, vmem, pl.BlockSpec(memory_space=pl.ANY)],
        out_specs=(vmem, vmem),
        scratch_shapes=[
            pltpu.VMEM(block_values.shape, jnp.float32),
            ext, ext, ext, ext,
            pltpu.VMEM((2, rows * PACK, 2 * bs // PACK * bs), jnp.bfloat16),
            pltpu.VMEM((2 * bs // PACK * bs, bs), jnp.bfloat16),
            pltpu.SMEM((rows * slots,), jnp.int32),
            pltpu.VMEM((rows, width, bs), jnp.float32),
            pltpu.VMEM((width, bs), jnp.float32),
            pltpu.VMEM((n, width, bs), jnp.float32),
            pltpu.SemaphoreType.DMA((chunks,)),
            pltpu.SemaphoreType.DMA((2, 2, 4)),
            pltpu.SemaphoreType.DMA((2, 2, 4)),
            pltpu.SemaphoreType.DMA((n,)),
            pltpu.SemaphoreType.DMA((n,)),
        ],
        compiler_params=pltpu.CompilerParams(
            collective_id=0, has_side_effects=True, vmem_limit_bytes=60 * 1024 * 1024
        ),
    )(shifts, block_cols, live_slots, needed[0], p_start, r_start, diag_shift, block_values)


def solution(mesh):
    return jax.shard_map(
        functools.partial(per_device, mesh.shape["group"], mesh.shape["dom"]),
        mesh=mesh,
        in_specs=(
            P(("group", "dom"), None),
            P(("group", "dom"), None),
            P(("group", "dom"), None),
            P(),
            P(("group", "dom"), None, None, None),
            P(("group", "dom"), None),
            P(("group", "dom")),
            P(("group", "dom"), None, None),
        ),
        out_specs=(P(None, ("group", "dom"), None), P()),
        check_vma=False,
    )
```

profile of v0, /device:TPU:0, one launch (start us, length us, event | category | flops | bytes accessed | tf_op | source)
XLA Modules:
  0.0 79.4 jit_solution(5873302630853028692)
XLA Ops:
  0.6 1.4 %copy.10.cols = s32[32,6]{1,0:T(8,128)} copy(s32[32,6]{0,1:T(8,128)} %param.13) | data formatting | bytes 1536 | tf_op args[5]
  2.0 74.4 %shard_map.95 = (f32[17,32,128]{2,1,0:T(8,128)}, f32[17,17]{1,0:T(8,128)}) custom-call(f32[8]{0:T(128)} %shifts.1, s32[32,6]{1,0:T(8,128)} %copy.10.cols, s32[32]{0:T(128)} %live.1, s32[4,16]{1,0:T(4,128)} %bitcast.1, f32[32,128]{1,0:T(8,128)} %p0.1, f32[32,128]{1,0:T(8,128)} %r0.1, f32[32,128]{1,0:T(8,128)} %diag.1, f32[32,6,128,128]{3,2,1,0:T(8,128)} %a_hbm.1), custom_call_target="tpu_custom_call" | custom-call | tf_op jit(solution)/shard_map/pallas_call | solution.py:250
  76.4 1.7 %copy.13 = f32[17,32,128]{2,1,0:T(8,128)} copy(f32[17,32,128]{2,1,0:T(8,128)} %get-tuple-element.4) | data formatting | bytes 557056
  78.0 1.3 %copy.14 = f32[17,17]{1,0:T(8,128)} copy(f32[17,17]{1,0:T(8,128)} %get-tuple-element.5) | data formatting | bytes 2312
where the time goes:
time: 79.7 us; the launch traced here: 79.4 us
  Pallas kernels  74.4 us (93%)
  local copies, waits for them, and re-layouts  4.36 us (5%)
    pallas_call x1, Pallas kernels, per_device(): pl.pallas_call(functools.partial(kernel, n_group, n_dom), out_shape=(jax....  74.4 us
    unnamed x3, local copies, waits for them, and re-layouts  4.36 us

commit v1 on v0

v1 whole, which is shorter than its diff:
```python
import functools

import jax
import jax.numpy as jnp
from jax import lax
from jax.experimental import pallas as pl
from jax.experimental.pallas import tpu as pltpu
from jax.sharding import PartitionSpec as P

MESH = pl.DeviceIdType.MESH
SUB = 8
PACK = 32


def split(x):
    hi = x.astype(jnp.bfloat16)
    lo = (x - hi.astype(jnp.float32)).astype(jnp.bfloat16)
    return hi, lo


def kernel(n_group, n_dom, shifts_h, cols_h, live_h, needed_h, p_h, r_h, diag_h, a_h, basis, gram,
           shifts, cols, live, needed, a_v, xp0, xp1, xr0, xr1, y0, diag, idx, fields, g_own, g_all, row_own, row_all,
           in_sem, a_sem, send_sem, recv_sem, g_send, g_recv, w_send, w_recv):
    rows, slots, bs, _ = a_v.shape
    depth = shifts.shape[0]
    halo = needed.shape[1]
    count = basis.shape[0]
    width = fields.shape[1]
    loads = a_sem.shape[0]
    per = rows // loads
    groups = rows // SUB
    zero_row = 5 * rows
    n = n_group * n_dom
    g, m = lax.axis_index("group"), lax.axis_index("dom")
    me = g * n_dom + m

    xs = ((xp0, xp1), (xr0, xr1))
    for which in range(2):
        for par in range(2):
            xs[which][par][pl.ds(rows, 2 * rows), :] = jnp.zeros((2 * rows, bs), jnp.float32)
            xs[which][par][pl.ds(zero_row, SUB), :] = jnp.zeros((SUB, bs), jnp.float32)

    barrier = pltpu.get_barrier_semaphore()

    def greet(d, carry):
        to = lax.rem(me + d, n)
        pl.semaphore_signal(barrier, inc=1, device_id=(to // n_dom, lax.rem(to, n_dom)), device_id_type=MESH)
        return carry

    lax.fori_loop(1, n, greet, 0)

    own = pl.ds(0, rows)
    small = (
        (cols_h, cols), (live_h, live), (needed_h, needed), (shifts_h, shifts),
        (p_h, xp0.at[own]), (r_h, xr0.at[own]), (diag_h, diag),
    )

    def small_copy(i):
        return pltpu.make_async_copy(small[i][0], small[i][1], in_sem.at[i])

    def chunk(c):
        part = pl.ds(c * per, per)
        return pltpu.make_async_copy(a_h.at[part], a_v.at[part], a_sem.at[c])

    for i in (4, 5, 0, 1, 2, 3, 6):
        small_copy(i).start()
    for c in range(loads):
        chunk(c).start()

    fields[...] = jnp.zeros_like(fields)

    peers = (
        (g, lax.rem(m + 1, n_dom)),
        (g, lax.rem(m + n_dom - 1, n_dom)),
        (lax.rem(g + 1, n_group), m),
        (lax.rem(g + n_group - 1, n_group), m),
    )

    def copy(which, par, q, k):
        return pltpu.make_async_remote_copy(
            src_ref=xs[which][par].at[pl.ds(q * SUB, SUB)],
            dst_ref=xs[which][par].at[pl.ds((1 + k) * rows + q * SUB, SUB)],
            send_sem=send_sem.at[which, par, q, k],
            recv_sem=recv_sem.at[which, par, q, k],
            device_id=peers[k],
            device_id_type=MESH,
        )

    def guarded(ok, fn):
        if ok is None:
            fn()
        else:
            pl.when(ok)(fn)

    sends = (m < n_dom - 1, m > 0, None, None)
    recvs = (m > 0, m < n_dom - 1, None, None)
    order = (2, 3, 0, 1)

    def both(x, y):
        if x is None:
            return y
        return x if y is None else jnp.logical_and(x, y)

    def start(which, par, q, ok=None):
        for k in order:
            guarded(both(ok, sends[k]), lambda k=k: copy(which, par, q, k).start())

    def wait_send(which, par, ok=None):
        for q in range(groups):
            for k in order:
                guarded(both(ok, sends[k]), lambda q=q, k=k: copy(which, par, q, k).wait_send())

    def wait_recv(which, par):
        for k in (0, 1, 2, 3):
            for q in range(groups):
                guarded(recvs[k], lambda q=q, k=k: copy(which, par, q, k).wait_recv())

    small_copy(4).wait()
    small_copy(5).wait()
    pl.semaphore_wait(barrier, n - 1)
    for which in range(2):
        for q in range(groups):
            start(which, 0, q)

    for i in (0, 1, 2, 3, 6):
        small_copy(i).wait()

    def place(b, carry):
        for s in range(1, slots):
            c = cols[s, b]
            e = jnp.maximum(c - rows, 0)
            k = e // halo
            far = (1 + k) * rows + needed[k, lax.rem(e, halo)]
            at = jnp.where(c < rows, c, far)
            idx[b * slots + s] = jnp.where(s < live[b], at, zero_row)
        return carry

    lax.fori_loop(0, rows, place, 0)

    for which in range(2):
        x = xs[which][0][own, :]
        basis[which * (depth + 1)] = x
        fields[:, which * (depth + 1), :] = x

    def reduced(accs):
        parts = [jnp.transpose(a).reshape(bs // SUB, SUB, bs).sum(axis=0) for a in accs]
        return jnp.stack(parts).sum(axis=1)

    def before(which, par, theta):
        for q in range(groups):
            at = pl.ds(q * SUB, SUB)
            x = xs[which][par][at, :]
            accs = []
            for i in range(SUB):
                b = q * SUB + i
                accs.append(a_v[b, 0] * xs[which][par][pl.ds(b, 1), :])
            y0[which, at, :] = reduced(accs) + (diag[at, :] - theta) * x

    def main(which, par, column, more):
        for q in range(groups):
            at = pl.ds(q * SUB, SUB)
            accs = []
            for i in range(SUB):
                b = q * SUB + i
                acc = None
                for s in range(1, slots):
                    term = a_v[b, s] * xs[which][par][pl.ds(idx[b * slots + s], 1), :]
                    acc = term if acc is None else acc + term
                accs.append(acc)
            y = reduced(accs) + y0[which, at, :]
            if more:
                xs[which][1 - par][at, :] = y
                start(which, 1 - par, q)
            basis[column, at, :] = y
            if more or which == 1:
                fields[at, column, :] = y

    for c in range(loads):
        chunk(c).wait()
    for which in range(2):
        before(which, 0, shifts[0])

    def turn(which, k, par, more, later):
        wait_recv(which, par)
        wait_send(which, 1 - par, later)
        main(which, par, which * (depth + 1) + k, more)
        if more:
            before(which, 1 - par, shifts[k])

    def two(t, carry):
        for par in range(2):
            for which in range(2):
                turn(which, 2 * t + 1 + par, par, True, t > 0 if par == 0 else None)
        return carry

    trips = (depth - 2) // 2
    lax.fori_loop(0, trips, two, 0)
    for k in range(2 * trips + 1, depth):
        for which in range(2):
            turn(which, k, (k - 1) % 2, which == 0 or k < depth - 1, None)

    acc = None
    for b in range(rows):
        hi, lo = split(fields[b])
        pair = jnp.concatenate([hi, lo], axis=0)
        term = lax.dot_general(pair, pair, (((1,), (1,)), ((), ())), preferred_element_type=jnp.float32)
        acc = term if acc is None else acc + term
    top = acc[:width] + acc[width:]
    part = top[:, :width] + top[:, width:]
    wide = jnp.concatenate([part, jnp.zeros((width, bs - width), jnp.float32)], axis=1)
    packed = wide[:SUB]
    for t in range(1, -(-count // SUB)):
        packed = packed + pltpu.roll(wide[t * SUB:(t + 1) * SUB], t * PACK, 1)
    g_own[...] = packed

    def share(d, src, dst, ssem, rsem):
        to = lax.rem(me + d, n)
        return pltpu.make_async_remote_copy(
            src_ref=src, dst_ref=dst.at[me], send_sem=ssem.at[d], recv_sem=rsem.at[me],
            device_id=(to // n_dom, lax.rem(to, n_dom)), device_id_type=MESH,
        )

    def arrival(d, src, dst, ssem, rsem):
        source = lax.rem(me + d, n)
        return pltpu.make_async_remote_copy(
            src_ref=src, dst_ref=dst.at[source], send_sem=ssem.at[0], recv_sem=rsem.at[source],
            device_id=(source // n_dom, lax.rem(source, n_dom)), device_id_type=MESH,
        )

    def each(fn):
        def body(d, carry):
            fn(d)
            return carry
        lax.fori_loop(1, n, body, 0)

    first = (g_own, g_all, g_send, g_recv)
    second = (row_own, row_all, w_send, w_recv)
    each(lambda d: share(d, *first).start())
    g_all[me] = g_own[...]

    wait_recv(0, (depth - 1) % 2)
    main(0, (depth - 1) % 2, depth, False)
    last = basis[depth].reshape(groups, SUB, bs)
    sums = []
    for j in range(width):
        if j < count:
            sums.append((last * basis[j].reshape(groups, SUB, bs)).sum(axis=0))
        else:
            sums.append(jnp.zeros((SUB, bs), jnp.float32))
    flat = jnp.stack(sums).sum(axis=1)
    full = jnp.concatenate([flat, jnp.zeros((bs - width, bs), jnp.float32)], axis=0)
    line = jnp.transpose(full).sum(axis=0, keepdims=True)
    row_own[...] = line
    each(lambda d: share(d, *second).start())
    row_all[me] = line

    each(lambda d: arrival(d, *first).wait_recv())
    total = lax.fori_loop(1, n, lambda i, t: t + g_all[i], g_all[0])
    pieces = [total] + [pltpu.roll(total, bs - t * PACK, 1) for t in range(1, -(-count // SUB))]
    table = jnp.concatenate(pieces, axis=0)
    r_id = lax.broadcasted_iota(jnp.int32, table.shape, 0)
    c_id = lax.broadcasted_iota(jnp.int32, table.shape, 1)
    each(lambda d: arrival(d, *second).wait_recv())
    sweep = row_all[...].reshape(n, bs).sum(axis=0, keepdims=True)
    spread = jnp.broadcast_to(sweep, table.shape)
    side = jnp.where(r_id == c_id, spread, 0.0).sum(axis=1, keepdims=True)
    table = jnp.where(r_id == depth, spread, jnp.where(c_id == depth, side, table))
    gram[...] = table[:count, :count] * (1.0 / (n * rows * bs))

    wait_send(0, 0)
    wait_send(0, 1)
    wait_send(1, (depth - 2) % 2)
    each(lambda d: share(d, *first).wait_send())
    each(lambda d: share(d, *second).wait_send())


def per_device(n_group, n_dom, p_start, r_start, diag_shift, shifts, block_values, block_cols, live_slots, needed):
    rows, bs = p_start.shape
    slots = block_values.shape[1]
    depth = shifts.shape[0]
    halo = needed.shape[2]
    columns = 2 * depth + 1
    width = -(-columns // SUB) * SUB
    n = n_group * n_dom
    loads = rows // 4
    groups = rows // SUB
    hbm = pl.BlockSpec(memory_space=pl.ANY)
    vmem = pl.BlockSpec(memory_space=pltpu.VMEM)
    ext = pltpu.VMEM((5 * rows + SUB, bs), jnp.float32)
    return pl.pallas_call(
        functools.partial(kernel, n_group, n_dom),
        out_shape=(
            jax.ShapeDtypeStruct((columns, rows, bs), jnp.float32),
            jax.ShapeDtypeStruct((columns, columns), jnp.float32),
        ),
        in_specs=[hbm] * 8,
        out_specs=(vmem, vmem),
        scratch_shapes=[
            pltpu.SMEM((depth,), jnp.float32),
            pltpu.SMEM((slots, rows), jnp.int32),
            pltpu.SMEM((rows,), jnp.int32),
            pltpu.SMEM((4, halo), jnp.int32),
            pltpu.VMEM(block_values.shape, jnp.float32),
            ext, ext, ext, ext,
            pltpu.VMEM((2, rows, bs), jnp.float32),
            pltpu.VMEM((rows, bs), jnp.float32),
            pltpu.SMEM((rows * slots,), jnp.int32),
            pltpu.VMEM((rows, width, bs), jnp.float32),
            pltpu.VMEM((SUB, bs), jnp.float32),
            pltpu.VMEM((n, SUB, bs), jnp.float32),
            pltpu.VMEM((1, bs), jnp.float32),
            pltpu.VMEM((n, 1, bs), jnp.float32),
            pltpu.SemaphoreType.DMA((7,)),
            pltpu.SemaphoreType.DMA((loads,)),
            pltpu.SemaphoreType.DMA((2, 2, groups, 4)),
            pltpu.SemaphoreType.DMA((2, 2, groups, 4)),
            pltpu.SemaphoreType.DMA((n,)),
            pltpu.SemaphoreType.DMA((n,)),
            pltpu.SemaphoreType.DMA((n,)),
            pltpu.SemaphoreType.DMA((n,)),
        ],
        compiler_params=pltpu.CompilerParams(
            collective_id=0, has_side_effects=True, vmem_limit_bytes=60 * 1024 * 1024
        ),
    )(shifts, block_cols.T, live_slots, needed[0], p_start, r_start, diag_shift, block_values)


def solution(mesh):
    return jax.shard_map(
        functools.partial(per_device, mesh.shape["group"], mesh.shape["dom"]),
        mesh=mesh,
        in_specs=(
            P(("group", "dom"), None),
            P(("group", "dom"), None),
            P(("group", "dom"), None),
            P(),
            P(("group", "dom"), None, None, None),
            P(("group", "dom"), None),
            P(("group", "dom")),
            P(("group", "dom"), None, None),
        ),
        out_specs=(P(None, ("group", "dom"), None), P()),
        check_vma=False,
    )
```

time: 79.7 us -> 52.7 us (0.66)
  Pallas kernels: 74.4 us -> 48.9 us
  local copies, waits for them, and re-layouts: 4.36 us -> 2.99 us
    pallas_call x1, Pallas kernels: 74.4 us -> 48.9 us  [per_device(): pl.pallas_call(functools.partial(kernel, n_group, n_dom), out_shape=(jax....]
    unnamed x3 -> x2, local copies, waits for them, and re-layouts: 4.36 us -> 2.99 us
where the time goes in v1:
time: 52.7 us; the launch traced here: 52.5 us
  Pallas kernels  48.9 us (93%)
  local copies, waits for them, and re-layouts  2.99 us (6%)
  between operations  0.64 us (1%)
    pallas_call x1, Pallas kernels, per_device(): pl.pallas_call(functools.partial(kernel, n_group, n_dom), out_shape=(jax....  48.9 us
    unnamed x2, local copies, waits for them, and re-layouts  2.99 us

profile of v1, /device:TPU:0, one launch (start us, length us, event | category | flops | bytes accessed | tf_op | source)
XLA Modules:
  0.0 52.5 jit_solution(3468891992039533583)
XLA Ops:
  0.6 48.9 %shard_map.95 = (f32[17,32,128]{2,1,0:T(8,128)}, f32[17,17]{1,0:T(8,128)}) custom-call(f32[8]{0:T(128)} %shifts_h.1, s32[6,32]{1,0:T(8,128)} %bitcast.2, s32[32]{0:T(128)} %live_h.1, s32[4,16]{1,0:T(4,128)} %bitcast.3, f32[32,128]{1,0:T(8,128)} %p_h.1, f32[32,128]{1,0:T(8,128)} %r_h.1, f32[32,128]{1,0:T(8,128)} %diag_h.1, f32[32,6,128,128]{3,2,1,0:T(8,128)} %a_h.1), custom_call_target="tpu_custom_call" | custom-call | tf_op jit(solution)/shard_map/pallas_call | solution.py:290
  49.5 1.7 %copy.12 = f32[17,32,128]{2,1,0:T(8,128)} copy(f32[17,32,128]{2,1,0:T(8,128)} %get-tuple-element.4) | data formatting | bytes 557056
  51.2 1.3 %copy.13 = f32[17,17]{1,0:T(8,128)} copy(f32[17,17]{1,0:T(8,128)} %get-tuple-element.5) | data formatting | bytes 2312

commit v2 on v1

v2 whole, which is shorter than its diff:
```python
import functools

import jax
import jax.numpy as jnp
from jax import lax
from jax.experimental import pallas as pl
from jax.experimental.pallas import tpu as pltpu
from jax.sharding import PartitionSpec as P

MESH = pl.DeviceIdType.MESH
SUB = 8
PACK = 32


def split(x):
    hi = x.astype(jnp.bfloat16)
    lo = (x - hi.astype(jnp.float32)).astype(jnp.bfloat16)
    return hi, lo


def kernel(n_group, n_dom, shifts_h, cols_h, live_h, needed_h, p_h, r_h, diag_h, a_h, basis, gram,
           shifts, cols, live, needed, a_v, xp0, xp1, xr0, xr1, y0, diag, idx, fields, g_own, g_all, row_own, row_all,
           in_sem, a_sem, send_sem, recv_sem, g_send, g_recv):
    rows, slots, bs, _ = a_v.shape
    depth = shifts.shape[0]
    halo = needed.shape[1]
    count = basis.shape[0]
    width = fields.shape[1]
    groups = rows // SUB
    zero_row = 5 * rows
    n = n_group * n_dom
    g, m = lax.axis_index("group"), lax.axis_index("dom")
    me = g * n_dom + m

    xs = ((xp0, xp1), (xr0, xr1))
    for which in range(2):
        for par in range(2):
            xs[which][par][pl.ds(rows, 2 * rows), :] = jnp.zeros((2 * rows, bs), jnp.float32)
            xs[which][par][pl.ds(zero_row, SUB), :] = jnp.zeros((SUB, bs), jnp.float32)

    peers = (
        (g, lax.rem(m + 1, n_dom)),
        (g, lax.rem(m + n_dom - 1, n_dom)),
        (lax.rem(g + 1, n_group), m),
        (lax.rem(g + n_group - 1, n_group), m),
    )
    sends = (m < n_dom - 1, m > 0, None, None)
    order = (2, 3, 0, 1)
    inner = jnp.logical_and(m > 0, m < n_dom - 1)
    others = [(a, b) for a in range(n_group) for b in range(n_dom) if a + b > 0]

    def at_offset(a, b):
        return lax.rem(g + a, n_group), lax.rem(m + b, n_dom)

    def guarded(ok, fn):
        if ok is None:
            fn()
        else:
            pl.when(ok)(fn)

    barrier = pltpu.get_barrier_semaphore()
    near = n_dom - 1 + n_group // 2 <= depth + 1
    if near:
        for k in order:
            guarded(sends[k], lambda k=k: pl.semaphore_signal(
                barrier, inc=1, device_id=peers[k], device_id_type=MESH))
    else:
        for a, b in others:
            pl.semaphore_signal(barrier, inc=1, device_id=at_offset(a, b), device_id_type=MESH)

    own = pl.ds(0, rows)
    small = (
        (p_h, xp0.at[own]), (r_h, xr0.at[own]), (cols_h, cols), (live_h, live), (needed_h, needed),
        (shifts_h, shifts), (diag_h, diag),
    )

    def small_copy(i):
        return pltpu.make_async_copy(small[i][0], small[i][1], in_sem.at[i])

    def chunk(c):
        part = pl.ds(0, 1) if c == 0 else pl.ds(1, slots - 1)
        return pltpu.make_async_copy(a_h.at[:, part], a_v.at[:, part], a_sem.at[c])

    for i in range(len(small)):
        small_copy(i).start()
    for c in range(2):
        chunk(c).start()

    def copy(which, par, q, k):
        return pltpu.make_async_remote_copy(
            src_ref=xs[which][par].at[pl.ds(q * SUB, SUB)],
            dst_ref=xs[which][par].at[pl.ds((1 + k) * rows + q * SUB, SUB)],
            send_sem=send_sem.at[which, par],
            recv_sem=recv_sem.at[which, par],
            device_id=peers[k],
            device_id_type=MESH,
        )

    def start(which, par, q):
        for k in order:
            guarded(sends[k], lambda k=k: copy(which, par, q, k).start())

    def halos(which, par, count):
        part = xs[which][par].at[pl.ds(rows, count * rows)]
        return pltpu.make_async_remote_copy(
            src_ref=part, dst_ref=part, send_sem=send_sem.at[which, par], recv_sem=recv_sem.at[which, par],
            device_id=peers[2], device_id_type=MESH,
        )

    def wait_send(which, par, ok=None):
        for count, side in ((4, inner), (3, jnp.logical_not(inner))):
            pl.when(side if ok is None else jnp.logical_and(ok, side))(
                lambda count=count: halos(which, par, count).wait_send())

    def wait_recv(which, par):
        for count, side in ((4, inner), (3, jnp.logical_not(inner))):
            pl.when(side)(lambda count=count: halos(which, par, count).wait_recv())

    fields[...] = jnp.zeros_like(fields)
    small_copy(0).wait()
    small_copy(1).wait()
    pl.semaphore_wait(barrier, jnp.where(inner, 4, 3) if near else n - 1)
    for which in range(2):
        for q in range(groups):
            start(which, 0, q)

    for i in range(2, len(small)):
        small_copy(i).wait()

    def place(b, carry):
        for s in range(1, slots):
            c = cols[s, b]
            e = jnp.maximum(c - rows, 0)
            k = e // halo
            far = (1 + k) * rows + needed[k, lax.rem(e, halo)]
            at = jnp.where(c < rows, c, far)
            idx[b * slots + s] = jnp.where(s < live[b], at, zero_row)
        return carry

    lax.fori_loop(0, rows, place, 0)

    for which in range(2):
        x = xs[which][0][own, :]
        basis[which * (depth + 1)] = x
        fields[:, which * (depth + 1), :] = x

    def folded(acc):
        return jnp.transpose(acc).reshape(bs // SUB, SUB, bs).sum(axis=0)

    def before(which, par, theta):
        x = xs[which][par]
        for q in range(groups):
            at = pl.ds(q * SUB, SUB)
            parts = [folded(a_v[q * SUB + i, 0] * x[pl.ds(q * SUB + i, 1), :]) for i in range(SUB)]
            y0[which, at, :] = jnp.stack(parts).sum(axis=1) + (diag[at, :] - theta) * x[at, :]

    def main(which, par, column, more):
        x = xs[which][par]

        def row(b):
            acc = None
            for s in range(1, slots):
                term = a_v[b, s] * x[pl.ds(idx[b * slots + s], 1), :]
                acc = term if acc is None else acc + term
            return folded(acc)

        def finish(q, parts):
            at = pl.ds(q * SUB, SUB)
            y = jnp.stack(parts).sum(axis=1) + y0[which, at, :]
            if more:
                xs[which][1 - par][at, :] = y
                start(which, 1 - par, q)
            basis[column, at, :] = y
            if more or which == 1:
                fields[at, column, :] = y

        held = None
        for q in range(groups):
            parts = []
            for i in range(SUB):
                parts.append(row(q * SUB + i))
                if held is not None and i == SUB // 2 - 1:
                    finish(q - 1, held)
            held = parts
        finish(groups - 1, held)

    chunk(0).wait()
    for which in range(2):
        before(which, 0, shifts[0])
    chunk(1).wait()

    def turn(which, k, par, more, later):
        wait_recv(which, par)
        wait_send(which, 1 - par, later)
        main(which, par, which * (depth + 1) + k, more)
        if more:
            before(which, 1 - par, shifts[k])

    def two(t, carry):
        for par in range(2):
            for which in range(2):
                turn(which, 2 * t + 1 + par, par, True, t > 0 if par == 0 else None)
        return carry

    trips = (depth - 2) // 2
    lax.fori_loop(0, trips, two, 0)
    for k in range(2 * trips + 1, depth):
        for which in range(2):
            turn(which, k, (k - 1) % 2, which == 0 or k < depth - 1, None)

    acc = None
    for b in range(rows):
        hi, lo = split(fields[b])
        pair = jnp.concatenate([hi, lo], axis=0)
        term = lax.dot_general(pair, pair, (((1,), (1,)), ((), ())), preferred_element_type=jnp.float32)
        acc = term if acc is None else acc + term
    top = acc[:width] + acc[width:]
    part = top[:, :width] + top[:, width:]
    wide = jnp.concatenate([part, jnp.zeros((width, bs - width), jnp.float32)], axis=1)
    packed = wide[:SUB]
    for t in range(1, -(-count // SUB)):
        packed = packed + pltpu.roll(wide[t * SUB:(t + 1) * SUB], t * PACK, 1)
    g_own[...] = packed

    def share(a, b, src, dst, i):
        return pltpu.make_async_remote_copy(
            src_ref=src, dst_ref=dst.at[me], send_sem=g_send.at[i], recv_sem=g_recv.at[i],
            device_id=at_offset(a, b), device_id_type=MESH,
        )

    def shared(dst, i):
        part = dst.at[pl.ds(0, n - 1)]
        return pltpu.make_async_remote_copy(
            src_ref=part, dst_ref=part, send_sem=g_send.at[i], recv_sem=g_recv.at[i],
            device_id=peers[2], device_id_type=MESH,
        )

    wait_recv(0, (depth - 1) % 2)
    for a, b in others:
        share(a, b, g_own, g_all, 0).start()
    g_all[me] = g_own[...]
    main(0, (depth - 1) % 2, depth, False)
    last = basis[depth].reshape(groups, SUB, bs)
    sums = []
    for j in range(width):
        if j < count:
            sums.append((last * basis[j].reshape(groups, SUB, bs)).sum(axis=0))
        else:
            sums.append(jnp.zeros((SUB, bs), jnp.float32))
    flat = jnp.stack(sums).sum(axis=1)
    full = jnp.concatenate([flat, jnp.zeros((bs - width, bs), jnp.float32)], axis=0)
    line = jnp.transpose(full).sum(axis=0, keepdims=True)
    row_own[...] = line
    for a, b in others:
        share(a, b, row_own, row_all, 1).start()
    row_all[me] = line

    shared(g_all, 0).wait_recv()
    total = g_all[...].sum(axis=0)
    pieces = [total] + [pltpu.roll(total, bs - t * PACK, 1) for t in range(1, -(-count // SUB))]
    table = jnp.concatenate(pieces, axis=0)
    r_id = lax.broadcasted_iota(jnp.int32, table.shape, 0)
    c_id = lax.broadcasted_iota(jnp.int32, table.shape, 1)
    shared(row_all, 1).wait_recv()
    sweep = row_all[...].reshape(n, bs).sum(axis=0, keepdims=True)
    spread = jnp.broadcast_to(sweep, table.shape)
    side = jnp.where(r_id == c_id, spread, 0.0).sum(axis=1, keepdims=True)
    table = jnp.where(r_id == depth, spread, jnp.where(c_id == depth, side, table))
    gram[...] = table[:count, :count] * (1.0 / (n * rows * bs))

    wait_send(0, 0)
    wait_send(0, 1)
    wait_send(1, (depth - 2) % 2)
    shared(g_all, 0).wait_send()
    shared(row_all, 1).wait_send()


def export(b_ref, g_ref, b_out, g_out, sem):
    copies = [pltpu.make_async_copy(b_ref, b_out, sem.at[0]), pltpu.make_async_copy(g_ref, g_out, sem.at[1])]
    for c in copies:
        c.start()
    for c in copies:
        c.wait()


def per_device(n_group, n_dom, p_start, r_start, diag_shift, shifts, block_values, block_cols, live_slots, needed):
    rows, bs = p_start.shape
    slots = block_values.shape[1]
    depth = shifts.shape[0]
    halo = needed.shape[2]
    columns = 2 * depth + 1
    width = -(-columns // SUB) * SUB
    n = n_group * n_dom
    hbm = pl.BlockSpec(memory_space=pltpu.HBM)
    vmem = pl.BlockSpec(memory_space=pltpu.VMEM)
    ext = pltpu.VMEM((5 * rows + SUB, bs), jnp.float32)
    basis, gram = pl.pallas_call(
        functools.partial(kernel, n_group, n_dom),
        out_shape=(
            jax.ShapeDtypeStruct((columns, rows, bs), jnp.float32),
            jax.ShapeDtypeStruct((columns, columns), jnp.float32),
        ),
        in_specs=[hbm] * 8,
        out_specs=(vmem, vmem),
        scratch_shapes=[
            pltpu.SMEM((depth,), jnp.float32),
            pltpu.SMEM((slots, rows), jnp.int32),
            pltpu.SMEM((rows,), jnp.int32),
            pltpu.SMEM((4, halo), jnp.int32),
            pltpu.VMEM(block_values.shape, jnp.float32),
            ext, ext, ext, ext,
            pltpu.VMEM((2, rows, bs), jnp.float32),
            pltpu.VMEM((rows, bs), jnp.float32),
            pltpu.SMEM((rows * slots,), jnp.int32),
            pltpu.VMEM((rows, width, bs), jnp.float32),
            pltpu.VMEM((SUB, bs), jnp.float32),
            pltpu.VMEM((n, SUB, bs), jnp.float32),
            pltpu.VMEM((1, bs), jnp.float32),
            pltpu.VMEM((n, 1, bs), jnp.float32),
            pltpu.SemaphoreType.DMA((7,)),
            pltpu.SemaphoreType.DMA((2,)),
            pltpu.SemaphoreType.DMA((2, 2)),
            pltpu.SemaphoreType.DMA((2, 2)),
            pltpu.SemaphoreType.DMA((2,)),
            pltpu.SemaphoreType.DMA((2,)),
        ],
        compiler_params=pltpu.CompilerParams(
            collective_id=0, has_side_effects=True, vmem_limit_bytes=24 * 1024 * 1024
        ),
    )(*[pltpu.with_memory_space_constraint(v, pltpu.HBM) for v in (
        shifts, block_cols.T, live_slots, needed[0], p_start, r_start, diag_shift, block_values)])
    return pl.pallas_call(
        export,
        out_shape=(
            jax.ShapeDtypeStruct(basis.shape, jnp.float32),
            jax.ShapeDtypeStruct(gram.shape, jnp.float32),
        ),
        in_specs=[vmem, vmem],
        out_specs=(hbm, hbm),
        scratch_shapes=[pltpu.SemaphoreType.DMA((2,))],
        compiler_params=pltpu.CompilerParams(vmem_limit_bytes=4 * 1024 * 1024),
    )(basis, gram)


def solution(mesh):
    return jax.shard_map(
        functools.partial(per_device, mesh.shape["group"], mesh.shape["dom"]),
        mesh=mesh,
        in_specs=(
            P(("group", "dom"), None),
            P(("group", "dom"), None),
            P(("group", "dom"), None),
            P(),
            P(("group", "dom"), None, None, None),
            P(("group", "dom"), None),
            P(("group", "dom")),
            P(("group", "dom"), None, None),
        ),
        out_specs=(P(None, ("group", "dom"), None), P()),
        check_vma=False,
    )
```

time: 52.7 us -> 43.9 us (0.83)
  Pallas kernels: 48.9 us -> 43.1 us
  local copies, waits for them, and re-layouts: 2.99 us -> 0 us
    pallas_call x1, Pallas kernels: 48.9 us -> 42.3 us  [per_device(): pl.pallas_call(functools.partial(kernel, n_group, n_dom), out_shape=(jax....]
    unnamed x2 -> x0, local copies, waits for them, and re-layouts: 2.99 us -> none
    pallas_call x0 -> x1, Pallas kernels: none -> 0.73 us  [per_device(): pl.pallas_call(export, out_shape=(jax.ShapeDtypeStruct(basis.shape, jnp.f...]
where the time goes in v2:
time: 43.9 us; the launch traced here: 43.7 us
  Pallas kernels  43.1 us (98%)
  between operations  0.64 us (1%)
    pallas_call x1, Pallas kernels, per_device(): pl.pallas_call(functools.partial(kernel, n_group, n_dom), out_shape=(jax....  42.3 us

profile of v2, /device:TPU:0, one launch (start us, length us, event | category | flops | bytes accessed | tf_op | source)
XLA Modules:
  0.0 43.7 jit_solution(1386285528295284586)
XLA Ops:
  0.6 42.3 %shard_map.95 = (f32[17,32,128]{2,1,0:T(8,128)S(1)}, f32[17,17]{1,0:T(8,128)S(1)}) custom-call(f32[8]{0:T(128)} %shifts_h.1, s32[6,32]{1,0:T(8,128)} %bitcast.2, s32[32]{0:T(128)} %live_h.1, s32[4,16]{1,0:T(4,128)} %bitcast.3, f32[32,128]{1,0:T(8,128)} %p_h.1, f32[32,128]{1,0:T(8,128)} %r_h.1, f32[32,128]{1,0:T(8,128)} %diag_h.1, f32[32,6,128,128]{3,2,1,0:T(8,128)} %a_h.1), custom_call_target="tpu_custom_call" | custom-call | tf_op jit(solution)/shard_map/pallas_call | solution.py:297
  43.0 0.7 %shard_map.96 = (f32[17,32,128]{2,1,0:T(8,128)}, f32[17,17]{1,0:T(8,128)}) custom-call(f32[17,32,128]{2,1,0:T(8,128)S(1)} %get-tuple-element.4.b_ref, f32[17,17]{1,0:T(8,128)S(1)} %get-tuple-element.5.g_ref), custom_call_target="tpu_custom_call" | custom-call | tf_op jit(solution)/shard_map/pallas_call | solution.py:332

commit v3 on v2

--- a/solution.py
+++ b/solution.py
@@ -10,6 +10,7 @@
 MESH = pl.DeviceIdType.MESH
 SUB = 8
 PACK = 32
+MXU_ROWS = 8
 
 
 def split(x):
@@ -19,7 +20,7 @@
 
 
 def kernel(n_group, n_dom, shifts_h, cols_h, live_h, needed_h, p_h, r_h, diag_h, a_h, basis, gram,
-           shifts, cols, live, needed, a_v, xp0, xp1, xr0, xr1, y0, diag, idx, fields, g_own, g_all, row_own, row_all,
+           shifts, cols, live, needed, a_v, w_v, xp0, xp1, xr0, xr1, y0, diag, idx, spot, fields, g_own, g_all, row_own, row_all,
            in_sem, a_sem, send_sem, recv_sem, g_send, g_recv):
     rows, slots, bs, _ = a_v.shape
     depth = shifts.shape[0]
@@ -47,7 +48,8 @@
     sends = (m < n_dom - 1, m > 0, None, None)
     order = (2, 3, 0, 1)
     inner = jnp.logical_and(m > 0, m < n_dom - 1)
-    others = [(a, b) for a in range(n_group) for b in range(n_dom) if a + b > 0]
+    others = [(a, b) for b in range(n_dom) for a in range(n_group) if a + b > 0]
+    others.sort(key=lambda o: -min(o[1], n_dom - o[1]))
 
     def at_offset(a, b):
         return lax.rem(g + a, n_group), lax.rem(m + b, n_dom)
@@ -59,9 +61,11 @@
             pl.when(ok)(fn)
 
     barrier = pltpu.get_barrier_semaphore()
-    near = n_dom - 1 + n_group // 2 <= depth + 1
+    near = n_dom <= depth
     if near:
-        for k in order:
+        for a in range(1, n_group):
+            pl.semaphore_signal(barrier, inc=1, device_id=at_offset(a, 0), device_id_type=MESH)
+        for k in (0, 1):
             guarded(sends[k], lambda k=k: pl.semaphore_signal(
                 barrier, inc=1, device_id=peers[k], device_id_type=MESH))
     else:
@@ -78,12 +82,16 @@
         return pltpu.make_async_copy(small[i][0], small[i][1], in_sem.at[i])
 
     def chunk(c):
-        part = pl.ds(0, 1) if c == 0 else pl.ds(1, slots - 1)
-        return pltpu.make_async_copy(a_h.at[:, part], a_v.at[:, part], a_sem.at[c])
+        part = (
+            (slice(None), pl.ds(0, 1)),
+            (pl.ds(0, MXU_ROWS), pl.ds(1, slots - 1)),
+            (pl.ds(MXU_ROWS, rows - MXU_ROWS), pl.ds(1, slots - 1)),
+        )[c]
+        return pltpu.make_async_copy(a_h.at[part], a_v.at[part], a_sem.at[c])
 
     for i in range(len(small)):
         small_copy(i).start()
-    for c in range(2):
+    for c in range(3):
         chunk(c).start()
 
     def copy(which, par, q, k):
@@ -119,25 +127,22 @@
     fields[...] = jnp.zeros_like(fields)
     small_copy(0).wait()
     small_copy(1).wait()
-    pl.semaphore_wait(barrier, jnp.where(inner, 4, 3) if near else n - 1)
+    pl.semaphore_wait(barrier, n_group + inner.astype(jnp.int32) if near else n - 1)
     for which in range(2):
         for q in range(groups):
             start(which, 0, q)
 
     for i in range(2, len(small)):
         small_copy(i).wait()
-
-    def place(b, carry):
+    for c in range(rows):
+        spot[c] = c
+    for k in range(4):
+        for h in range(halo):
+            spot[rows + k * halo + h] = (1 + k) * rows + needed[k, h]
+    for b in range(rows):
+        used = live[b]
         for s in range(1, slots):
-            c = cols[s, b]
-            e = jnp.maximum(c - rows, 0)
-            k = e // halo
-            far = (1 + k) * rows + needed[k, lax.rem(e, halo)]
-            at = jnp.where(c < rows, c, far)
-            idx[b * slots + s] = jnp.where(s < live[b], at, zero_row)
-        return carry
-
-    lax.fori_loop(0, rows, place, 0)
+            idx[b * slots + s] = jnp.where(s < used, spot[cols[s, b]], zero_row)
 
     for which in range(2):
         x = xs[which][0][own, :]
@@ -154,7 +159,7 @@
             parts = [folded(a_v[q * SUB + i, 0] * x[pl.ds(q * SUB + i, 1), :]) for i in range(SUB)]
             y0[which, at, :] = jnp.stack(parts).sum(axis=1) + (diag[at, :] - theta) * x[at, :]
 
-    def main(which, par, column, more):
+    def main(which, par, column, more, keep):
         x = xs[which][par]
 
         def row(b):
@@ -171,28 +176,69 @@
                 xs[which][1 - par][at, :] = y
                 start(which, 1 - par, q)
             basis[column, at, :] = y
-            if more or which == 1:
+            if keep:
                 fields[at, column, :] = y
 
-        held = None
-        for q in range(groups):
-            parts = []
-            for i in range(SUB):
-                parts.append(row(q * SUB + i))
-                if held is not None and i == SUB // 2 - 1:
-                    finish(q - 1, held)
-            held = parts
-        finish(groups - 1, held)
+        sub = lax.broadcasted_iota(jnp.int32, (SUB, bs), 0)
+
+        def pair(p):
+            acc = None
+            for s in range(1, slots):
+                v = jnp.where(
+                    sub < 2,
+                    x[pl.ds(idx[2 * p * slots + s], 1), :],
+                    x[pl.ds(idx[(2 * p + 1) * slots + s], 1), :],
+                )
+                hi = v.astype(jnp.bfloat16).astype(jnp.float32)
+                lhs = jnp.where(sub % 2 == 0, hi, v - hi).astype(jnp.bfloat16)
+                term = jnp.dot(
+                    jnp.concatenate([lhs, lhs], axis=1), w_v[p, s - 1], preferred_element_type=jnp.float32
+                )
+                acc = term if acc is None else acc + term
+            return [
+                jnp.where(sub < 2, acc[:, :bs], 0.0),
+                jnp.where(sub // 2 == 1, acc[:, bs:], 0.0),
+            ]
+
+        parts = {}
+        held = []
+        todo = list(range(MXU_ROWS, rows))
+        done = 0
+        for p in range(MXU_ROWS // 2):
+            parts[2 * p], parts[2 * p + 1] = pair(p)
+            stop = (p + 1) * len(todo) // (MXU_ROWS // 2) if p + 1 < MXU_ROWS // 2 else len(todo)
+            for b in todo[done:stop]:
+                parts[b] = row(b)
+                if b % SUB == SUB // 2 - 1 and held:
+                    finish(held[0], [parts[held[0] * SUB + i] for i in range(SUB)])
+                    held = held[1:]
+                if b % SUB == SUB - 1:
+                    held.append(b // SUB)
+            done = stop
+        for q in [h for h in held] + [q for q in range(groups) if (q + 1) * SUB <= MXU_ROWS]:
+            finish(q, [parts[q * SUB + i] for i in range(SUB)])
 
     chunk(0).wait()
     for which in range(2):
         before(which, 0, shifts[0])
     chunk(1).wait()
 
-    def turn(which, k, par, more, later):
+    def weights(p, carry):
+        for s in range(1, slots):
+            for e in range(2):
+                t = jnp.transpose(a_v[2 * p + e, s])
+                hi, lo = split(t)
+                w_v[p, s - 1, pl.ds(0, bs), pl.ds(e * bs, bs)] = hi
+                w_v[p, s - 1, pl.ds(bs, bs), pl.ds(e * bs, bs)] = lo
+        return carry
+
+    lax.fori_loop(0, MXU_ROWS // 2, weights, 0)
+    chunk(2).wait()
+
+    def turn(which, k, par, more, later, keep=True):
         wait_recv(which, par)
         wait_send(which, 1 - par, later)
-        main(which, par, which * (depth + 1) + k, more)
+        main(which, par, which * (depth + 1) + k, more, keep)
         if more:
             before(which, 1 - par, shifts[k])
 
@@ -204,10 +250,24 @@
 
     trips = (depth - 2) // 2
     lax.fori_loop(0, trips, two, 0)
-    for k in range(2 * trips + 1, depth):
+    for k in range(2 * trips + 1, depth - 1):
         for which in range(2):
             turn(which, k, (k - 1) % 2, which == 0 or k < depth - 1, None)
 
+    def share(a, b, src, dst, i):
+        return pltpu.make_async_remote_copy(
+            src_ref=src, dst_ref=dst.at[me], send_sem=g_send.at[i], recv_sem=g_recv.at[i],
+            device_id=at_offset(a, b), device_id_type=MESH,
+        )
+
+    def shared(dst, i):
+        part = dst.at[pl.ds(0, n - 1)]
+        return pltpu.make_async_remote_copy(
+            src_ref=part, dst_ref=part, send_sem=g_send.at[i], recv_sem=g_recv.at[i],
+            device_id=peers[2], device_id_type=MESH,
+        )
+
+    turn(0, depth - 1, depth % 2, True, None, False)
     acc = None
     for b in range(rows):
         hi, lo = split(fields[b])
@@ -222,34 +282,33 @@
         packed = packed + pltpu.roll(wide[t * SUB:(t + 1) * SUB], t * PACK, 1)
     g_own[...] = packed
 
-    def share(a, b, src, dst, i):
-        return pltpu.make_async_remote_copy(
-            src_ref=src, dst_ref=dst.at[me], send_sem=g_send.at[i], recv_sem=g_recv.at[i],
-            device_id=at_offset(a, b), device_id_type=MESH,
-        )
-
-    def shared(dst, i):
-        part = dst.at[pl.ds(0, n - 1)]
-        return pltpu.make_async_remote_copy(
-            src_ref=part, dst_ref=part, send_sem=g_send.at[i], recv_sem=g_recv.at[i],
-            device_id=peers[2], device_id_type=MESH,
-        )
-
-    wait_recv(0, (depth - 1) % 2)
     for a, b in others:
         share(a, b, g_own, g_all, 0).start()
     g_all[me] = g_own[...]
-    main(0, (depth - 1) % 2, depth, False)
-    last = basis[depth].reshape(groups, SUB, bs)
-    sums = []
-    for j in range(width):
-        if j < count:
-            sums.append((last * basis[j].reshape(groups, SUB, bs)).sum(axis=0))
-        else:
-            sums.append(jnp.zeros((SUB, bs), jnp.float32))
-    flat = jnp.stack(sums).sum(axis=1)
-    full = jnp.concatenate([flat, jnp.zeros((bs - width, bs), jnp.float32)], axis=0)
-    line = jnp.transpose(full).sum(axis=0, keepdims=True)
+    turn(1, depth - 1, depth % 2, False, None, False)
+
+    late = (depth - 1, 2 * depth, depth)
+
+    def products(c, known):
+        x = basis[c].reshape(groups, SUB, bs)
+        sums = []
+        for j in range(PACK):
+            if j in known:
+                sums.append((x * basis[j].reshape(groups, SUB, bs)).sum(axis=0))
+            else:
+                sums.append(jnp.zeros((SUB, bs), jnp.float32))
+        return jnp.stack(sums).sum(axis=1)
+
+    seen = [j for j in range(count) if j != depth]
+    halves = [products(late[0], seen), products(late[1], seen)]
+    early = jnp.transpose(jnp.concatenate(halves + [jnp.zeros((bs - 2 * PACK, bs), jnp.float32)], axis=0))
+    early = early.sum(axis=0, keepdims=True)
+
+    wait_recv(0, (depth - 1) % 2)
+    main(0, (depth - 1) % 2, depth, False, False)
+    pad = jnp.zeros((2 * PACK, bs), jnp.float32)
+    end = jnp.concatenate([pad, products(depth, list(range(count))), pad[:bs - 3 * PACK]], axis=0)
+    line = jnp.transpose(end).sum(axis=0, keepdims=True) + early
     row_own[...] = line
     for a, b in others:
         share(a, b, row_own, row_all, 1).start()
@@ -262,10 +321,12 @@
     r_id = lax.broadcasted_iota(jnp.int32, table.shape, 0)
     c_id = lax.broadcasted_iota(jnp.int32, table.shape, 1)
     shared(row_all, 1).wait_recv()
-    sweep = row_all[...].reshape(n, bs).sum(axis=0, keepdims=True)
-    spread = jnp.broadcast_to(sweep, table.shape)
-    side = jnp.where(r_id == c_id, spread, 0.0).sum(axis=1, keepdims=True)
-    table = jnp.where(r_id == depth, spread, jnp.where(c_id == depth, side, table))
+    sweep = jnp.broadcast_to(row_all[...].reshape(n, bs).sum(axis=0, keepdims=True), table.shape)
+    for i in (1, 0, 2):
+        c = late[i]
+        across = sweep if i == 0 else pltpu.roll(sweep, bs - i * PACK, 1)
+        down = jnp.where(c_id == r_id + i * PACK, sweep, 0.0).sum(axis=1, keepdims=True)
+        table = jnp.where(r_id == c, across, jnp.where(c_id == c, down, table))
     gram[...] = table[:count, :count] * (1.0 / (n * rows * bs))
 
     wait_send(0, 0)
@@ -308,17 +369,19 @@
             pltpu.SMEM((rows,), jnp.int32),
             pltpu.SMEM((4, halo), jnp.int32),
             pltpu.VMEM(block_values.shape, jnp.float32),
+            pltpu.VMEM((MXU_ROWS // 2, slots - 1, 2 * bs, 2 * bs), jnp.bfloat16),
             ext, ext, ext, ext,
             pltpu.VMEM((2, rows, bs), jnp.float32),
             pltpu.VMEM((rows, bs), jnp.float32),
             pltpu.SMEM((rows * slots,), jnp.int32),
+            pltpu.SMEM((rows + 4 * halo,), jnp.int32),
             pltpu.VMEM((rows, width, bs), jnp.float32),
             pltpu.VMEM((SUB, bs), jnp.float32),
             pltpu.VMEM((n, SUB, bs), jnp.float32),
             pltpu.VMEM((1, bs), jnp.float32),
             pltpu.VMEM((n, 1, bs), jnp.float32),
             pltpu.SemaphoreType.DMA((7,)),
-            pltpu.SemaphoreType.DMA((2,)),
+            pltpu.SemaphoreType.DMA((3,)),
             pltpu.SemaphoreType.DMA((2, 2)),
             pltpu.SemaphoreType.DMA((2, 2)),
             pltpu.SemaphoreType.DMA((2,)),

time: 43.9 us -> 43.4 us (0.989)
  Pallas kernels: 43.1 us -> 42.5 us
    pallas_call x1, Pallas kernels: 42.3 us -> 41.7 us  [per_device(): pl.pallas_call(functools.partial(kernel, n_group, n_dom), out_shape=(jax....]
where the time goes in v3:
time: 43.4 us; the launch traced here: 43.1 us
  Pallas kernels  42.5 us (98%)
  between operations  0.64 us (1%)
    pallas_call x1, Pallas kernels, per_device(): pl.pallas_call(functools.partial(kernel, n_group, n_dom), out_shape=(jax....  41.7 us

profile of v3, /device:TPU:0, one launch (start us, length us, event | category | flops | bytes accessed | tf_op | source)
XLA Modules:
  0.0 43.1 jit_solution(14889681435237572363)
XLA Ops:
  0.6 41.7 %shard_map.95 = (f32[17,32,128]{2,1,0:T(8,128)S(1)}, f32[17,17]{1,0:T(8,128)S(1)}) custom-call(f32[8]{0:T(128)} %shifts_h.1, s32[6,32]{1,0:T(8,128)} %bitcast.2, s32[32]{0:T(128)} %live_h.1, s32[4,16]{1,0:T(4,128)} %bitcast.3, f32[32,128]{1,0:T(8,128)} %p_h.1, f32[32,128]{1,0:T(8,128)} %r_h.1, f32[32,128]{1,0:T(8,128)} %diag_h.1, f32[32,6,128,128]{3,2,1,0:T(8,128)} %a_h.1), custom_call_target="tpu_custom_call" | custom-call | tf_op jit(solution)/shard_map/pallas_call | solution.py:358
  42.4 0.7 %shard_map.96 = (f32[17,32,128]{2,1,0:T(8,128)}, f32[17,17]{1,0:T(8,128)}) custom-call(f32[17,32,128]{2,1,0:T(8,128)S(1)} %get-tuple-element.4.b_ref, f32[17,17]{1,0:T(8,128)S(1)} %get-tuple-element.5.g_ref), custom_call_target="tpu_custom_call" | custom-call | tf_op jit(solution)/shard_map/pallas_call | solution.py:395

commit v4 on v3

--- a/solution.py
+++ b/solution.py
@@ -20,8 +20,8 @@
 
 
 def kernel(n_group, n_dom, shifts_h, cols_h, live_h, needed_h, p_h, r_h, diag_h, a_h, basis, gram,
-           shifts, cols, live, needed, a_v, w_v, xp0, xp1, xr0, xr1, y0, diag, idx, spot, fields, g_own, g_all, row_own, row_all,
-           in_sem, a_sem, send_sem, recv_sem, g_send, g_recv):
+           shifts, cols, live, needed, a_v, w_v, xp0, xp1, xr0, xr1, y0, diag, idx, spot, want, fresh, outbox, fields, g_own, g_all, row_own, row_all,
+           in_sem, a_sem, send_sem, recv_sem, g_send, g_recv, l_send, l_recv):
     rows, slots, bs, _ = a_v.shape
     depth = shifts.shape[0]
     halo = needed.shape[1]
@@ -39,6 +39,10 @@
             xs[which][par][pl.ds(rows, 2 * rows), :] = jnp.zeros((2 * rows, bs), jnp.float32)
             xs[which][par][pl.ds(zero_row, SUB), :] = jnp.zeros((SUB, bs), jnp.float32)
 
+    for k in range(2):
+        for h in range(halo):
+            want[k, k, h] = 0
+
     peers = (
         (g, lax.rem(m + 1, n_dom)),
         (g, lax.rem(m + n_dom - 1, n_dom)),
@@ -49,7 +53,7 @@
     order = (2, 3, 0, 1)
     inner = jnp.logical_and(m > 0, m < n_dom - 1)
     others = [(a, b) for b in range(n_dom) for a in range(n_group) if a + b > 0]
-    others.sort(key=lambda o: -min(o[1], n_dom - o[1]))
+    others.sort(key=lambda o: (o[1] == 0, o[1], -abs(o[0] - n_group / 2 + 0.5)))
 
     def at_offset(a, b):
         return lax.rem(g + a, n_group), lax.rem(m + b, n_dom)
@@ -94,55 +98,85 @@
     for c in range(3):
         chunk(c).start()
 
-    def copy(which, par, q, k):
+    def copy(which, par, k, whole):
+        if whole:
+            src, size = xs[which][par].at[own], rows
+        else:
+            src, size = outbox.at[which, par, pl.ds(k * halo, halo)], halo
         return pltpu.make_async_remote_copy(
-            src_ref=xs[which][par].at[pl.ds(q * SUB, SUB)],
-            dst_ref=xs[which][par].at[pl.ds((1 + k) * rows + q * SUB, SUB)],
+            src_ref=src,
+            dst_ref=xs[which][par].at[pl.ds((1 + k) * rows, size)],
             send_sem=send_sem.at[which, par],
             recv_sem=recv_sem.at[which, par],
             device_id=peers[k],
             device_id_type=MESH,
         )
 
-    def start(which, par, q):
+    def start(which, par, whole=False):
         for k in order:
-            guarded(sends[k], lambda k=k: copy(which, par, q, k).start())
+            guarded(sends[k], lambda k=k: copy(which, par, k, whole).start())
 
     def halos(which, par, count):
-        part = xs[which][par].at[pl.ds(rows, count * rows)]
+        part = xs[which][par].at[pl.ds(rows, count)]
         return pltpu.make_async_remote_copy(
             src_ref=part, dst_ref=part, send_sem=send_sem.at[which, par], recv_sem=recv_sem.at[which, par],
             device_id=peers[2], device_id_type=MESH,
         )
 
-    def wait_send(which, par, ok=None):
+    def both(x, y):
+        return y if x is None else jnp.logical_and(x, y)
+
+    def per_side(fn, whole, ok=None):
         for count, side in ((4, inner), (3, jnp.logical_not(inner))):
-            pl.when(side if ok is None else jnp.logical_and(ok, side))(
-                lambda count=count: halos(which, par, count).wait_send())
-
-    def wait_recv(which, par):
-        for count, side in ((4, inner), (3, jnp.logical_not(inner))):
-            pl.when(side)(lambda count=count: halos(which, par, count).wait_recv())
+            if whole is None or whole is False:
+                pl.when(both(ok, side))(lambda count=count: fn(count * halo))
+            elif whole is True:
+                pl.when(both(ok, side))(lambda count=count: fn(count * rows))
+            else:
+                pl.when(both(ok, jnp.logical_and(side, whole)))(lambda count=count: fn(count * rows))
+                pl.when(both(ok, jnp.logical_and(side, jnp.logical_not(whole))))(lambda count=count: fn(count * halo))
+
+    def wait_send(which, par, whole, ok=None):
+        per_side(lambda size: halos(which, par, size).wait_send(), whole, ok)
+
+    def wait_recv(which, par, whole):
+        per_side(lambda size: halos(which, par, size).wait_recv(), whole)
+
+    def list_copy(j):
+        return pltpu.make_async_remote_copy(
+            src_ref=needed, dst_ref=want.at[j], send_sem=l_send.at[j], recv_sem=l_recv.at[j],
+            device_id=peers[j ^ 1], device_id_type=MESH,
+        )
+
+    asks = (m > 0, m < n_dom - 1, None, None)
+    asked = sends
 
     fields[...] = jnp.zeros_like(fields)
     small_copy(0).wait()
     small_copy(1).wait()
     pl.semaphore_wait(barrier, n_group + inner.astype(jnp.int32) if near else n - 1)
+    small_copy(4).wait()
+    for j in range(4):
+        guarded(asks[j], lambda j=j: list_copy(j).start())
     for which in range(2):
-        for q in range(groups):
-            start(which, 0, q)
-
-    for i in range(2, len(small)):
+        start(which, 0, True)
+
+    for i in (2, 3, 5, 6):
         small_copy(i).wait()
+    wide = rows + 4 * halo
     for c in range(rows):
         spot[c] = c
+        spot[wide + c] = c
     for k in range(4):
         for h in range(halo):
             spot[rows + k * halo + h] = (1 + k) * rows + needed[k, h]
+            spot[wide + rows + k * halo + h] = (1 + k) * rows + h
     for b in range(rows):
         used = live[b]
         for s in range(1, slots):
-            idx[b * slots + s] = jnp.where(s < used, spot[cols[s, b]], zero_row)
+            c = cols[s, b]
+            idx[b * slots + s] = jnp.where(s < used, spot[c], zero_row)
+            idx[(rows + b) * slots + s] = jnp.where(s < used, spot[wide + c], zero_row)
 
     for which in range(2):
         x = xs[which][0][own, :]
@@ -159,13 +193,13 @@
             parts = [folded(a_v[q * SUB + i, 0] * x[pl.ds(q * SUB + i, 1), :]) for i in range(SUB)]
             y0[which, at, :] = jnp.stack(parts).sum(axis=1) + (diag[at, :] - theta) * x[at, :]
 
-    def main(which, par, column, more, keep):
+    def main(which, par, column, more, keep, base, first=None):
         x = xs[which][par]
 
         def row(b):
             acc = None
             for s in range(1, slots):
-                term = a_v[b, s] * x[pl.ds(idx[b * slots + s], 1), :]
+                term = a_v[b, s] * x[pl.ds(idx[base + b * slots + s], 1), :]
                 acc = term if acc is None else acc + term
             return folded(acc)
 
@@ -173,8 +207,8 @@
             at = pl.ds(q * SUB, SUB)
             y = jnp.stack(parts).sum(axis=1) + y0[which, at, :]
             if more:
+                fresh[which, at, :] = y
                 xs[which][1 - par][at, :] = y
-                start(which, 1 - par, q)
             basis[column, at, :] = y
             if keep:
                 fields[at, column, :] = y
@@ -186,8 +220,8 @@
             for s in range(1, slots):
                 v = jnp.where(
                     sub < 2,
-                    x[pl.ds(idx[2 * p * slots + s], 1), :],
-                    x[pl.ds(idx[(2 * p + 1) * slots + s], 1), :],
+                    x[pl.ds(idx[base + 2 * p * slots + s], 1), :],
+                    x[pl.ds(idx[base + (2 * p + 1) * slots + s], 1), :],
                 )
                 hi = v.astype(jnp.bfloat16).astype(jnp.float32)
                 lhs = jnp.where(sub % 2 == 0, hi, v - hi).astype(jnp.bfloat16)
@@ -200,27 +234,41 @@
                 jnp.where(sub // 2 == 1, acc[:, bs:], 0.0),
             ]
 
-        parts = {}
-        held = []
+        parts, born, done = {}, {}, set()
+
+        def close(q):
+            finish(q, [parts.pop(q * SUB + i) for i in range(SUB)])
+            done.add(q)
+
+        def settle(now, lag):
+            for q in range(groups):
+                mine = range(q * SUB, q * SUB + SUB)
+                if q not in done and all(b in parts for b in mine) and now - max(born[b] for b in mine) >= lag:
+                    close(q)
+
+        pairs = list(range(MXU_ROWS // 2))
         todo = list(range(MXU_ROWS, rows))
-        done = 0
-        for p in range(MXU_ROWS // 2):
-            parts[2 * p], parts[2 * p + 1] = pair(p)
-            stop = (p + 1) * len(todo) // (MXU_ROWS // 2) if p + 1 < MXU_ROWS // 2 else len(todo)
-            for b in todo[done:stop]:
-                parts[b] = row(b)
-                if b % SUB == SUB // 2 - 1 and held:
-                    finish(held[0], [parts[held[0] * SUB + i] for i in range(SUB)])
-                    held = held[1:]
-                if b % SUB == SUB - 1:
-                    held.append(b // SUB)
-            done = stop
-        for q in [h for h in held] + [q for q in range(groups) if (q + 1) * SUB <= MXU_ROWS]:
-            finish(q, [parts[q * SUB + i] for i in range(SUB)])
+        for i, b in enumerate(todo):
+            while pairs and i >= 0.8 * len(todo) * (MXU_ROWS // 2 - len(pairs)) / (MXU_ROWS // 2):
+                p = pairs.pop(0)
+                parts[2 * p], parts[2 * p + 1] = pair(p)
+                born[2 * p] = born[2 * p + 1] = i + 4
+            parts[b] = row(b)
+            born[b] = i
+            settle(i, 4)
+        settle(len(todo), -rows)
+        if more:
+            if first is not None and which == 0 and par == 0:
+                for j in range(4):
+                    pl.when(both(asked[j], first))(lambda j=j: list_copy(j).wait_recv())
+                    pl.when(both(asks[j], first))(lambda j=j: list_copy(j).wait_send())
+            for k in order:
+                for h in range(halo):
+                    outbox[which, 1 - par, pl.ds(k * halo + h, 1), :] = fresh[which, pl.ds(want[k, k, h], 1), :]
+                guarded(sends[k], lambda k=k: copy(which, 1 - par, k, False).start())
 
     chunk(0).wait()
-    for which in range(2):
-        before(which, 0, shifts[0])
+    before(0, 0, shifts[0])
     chunk(1).wait()
 
     def weights(p, carry):
@@ -235,17 +283,29 @@
     lax.fori_loop(0, MXU_ROWS // 2, weights, 0)
     chunk(2).wait()
 
-    def turn(which, k, par, more, later, keep=True):
-        wait_recv(which, par)
-        wait_send(which, 1 - par, later)
-        main(which, par, which * (depth + 1) + k, more, keep)
-        if more:
+    full = rows * slots
+
+    def turn(which, k, par, more, first, keep=True):
+        if which == 1:
+            before(which, par, shifts[k - 1])
+        if first is None:
+            wait_recv(which, par, False)
+            wait_send(which, 1 - par, False)
+        elif par == 0:
+            wait_recv(which, par, first)
+            wait_send(which, 1 - par, False, jnp.logical_not(first))
+        else:
+            wait_recv(which, par, False)
+            wait_send(which, 1 - par, first)
+        base = jnp.where(first, 0, full) if first is not None and par == 0 else full
+        main(which, par, which * (depth + 1) + k, more, keep, base, first)
+        if more and which == 0:
             before(which, 1 - par, shifts[k])
 
     def two(t, carry):
         for par in range(2):
             for which in range(2):
-                turn(which, 2 * t + 1 + par, par, True, t > 0 if par == 0 else None)
+                turn(which, 2 * t + 1 + par, par, True, t == 0)
         return carry
 
     trips = (depth - 2) // 2
@@ -304,8 +364,8 @@
     early = jnp.transpose(jnp.concatenate(halves + [jnp.zeros((bs - 2 * PACK, bs), jnp.float32)], axis=0))
     early = early.sum(axis=0, keepdims=True)
 
-    wait_recv(0, (depth - 1) % 2)
-    main(0, (depth - 1) % 2, depth, False, False)
+    wait_recv(0, (depth - 1) % 2, False)
+    main(0, (depth - 1) % 2, depth, False, False, full)
     pad = jnp.zeros((2 * PACK, bs), jnp.float32)
     end = jnp.concatenate([pad, products(depth, list(range(count))), pad[:bs - 3 * PACK]], axis=0)
     line = jnp.transpose(end).sum(axis=0, keepdims=True) + early
@@ -329,9 +389,9 @@
         table = jnp.where(r_id == c, across, jnp.where(c_id == c, down, table))
     gram[...] = table[:count, :count] * (1.0 / (n * rows * bs))
 
-    wait_send(0, 0)
-    wait_send(0, 1)
-    wait_send(1, (depth - 2) % 2)
+    wait_send(0, 0, False)
+    wait_send(0, 1, False)
+    wait_send(1, (depth - 2) % 2, False)
     shared(g_all, 0).wait_send()
     shared(row_all, 1).wait_send()
 
@@ -373,8 +433,11 @@
             ext, ext, ext, ext,
             pltpu.VMEM((2, rows, bs), jnp.float32),
             pltpu.VMEM((rows, bs), jnp.float32),
-            pltpu.SMEM((rows * slots,), jnp.int32),
-            pltpu.SMEM((rows + 4 * halo,), jnp.int32),
+            pltpu.SMEM((2 * rows * slots,), jnp.int32),
+            pltpu.SMEM((2 * (rows + 4 * halo),), jnp.int32),
+            pltpu.SMEM((4, 4, halo), jnp.int32),
+            pltpu.VMEM((2, rows, bs), jnp.float32),
+            pltpu.VMEM((2, 2, 4 * halo, bs), jnp.float32),
             pltpu.VMEM((rows, width, bs), jnp.float32),
             pltpu.VMEM((SUB, bs), jnp.float32),
             pltpu.VMEM((n, SUB, bs), jnp.float32),
@@ -386,6 +449,8 @@
             pltpu.SemaphoreType.DMA((2, 2)),
             pltpu.SemaphoreType.DMA((2,)),
             pltpu.SemaphoreType.DMA((2,)),
+            pltpu.SemaphoreType.DMA((4,)),
+            pltpu.SemaphoreType.DMA((4,)),
         ],
         compiler_params=pltpu.CompilerParams(
             collective_id=0, has_side_effects=True, vmem_limit_bytes=24 * 1024 * 1024

time: 43.4 us -> 43.4 us (level)
  no operation moved by 1% of the time
where the time goes in v4:
time: 43.4 us; the launch traced here: 43.1 us
  Pallas kernels  42.4 us (98%)
  between operations  0.64 us (1%)
    pallas_call x1, Pallas kernels, per_device(): pl.pallas_call(functools.partial(kernel, n_group, n_dom), out_shape=(jax....  41.7 us

profile of v4, /device:TPU:0, one launch (start us, length us, event | category | flops | bytes accessed | tf_op | source)
XLA Modules:
  0.0 43.1 jit_solution(873697313730754303)
XLA Ops:
  0.6 41.7 %shard_map.95 = (f32[17,32,128]{2,1,0:T(8,128)S(1)}, f32[17,17]{1,0:T(8,128)S(1)}) custom-call(f32[8]{0:T(128)} %shifts_h.1, s32[6,32]{1,0:T(8,128)} %bitcast.2, s32[32]{0:T(128)} %live_h.1, s32[4,16]{1,0:T(4,128)} %bitcast.3, f32[32,128]{1,0:T(8,128)} %p_h.1, f32[32,128]{1,0:T(8,128)} %r_h.1, f32[32,128]{1,0:T(8,128)} %diag_h.1, f32[32,6,128,128]{3,2,1,0:T(8,128)} %a_h.1), custom_call_target="tpu_custom_call" | custom-call | tf_op jit(solution)/shard_map/pallas_call | solution.py:418
  42.3 0.7 %shard_map.96 = (f32[17,32,128]{2,1,0:T(8,128)}, f32[17,17]{1,0:T(8,128)}) custom-call(f32[17,32,128]{2,1,0:T(8,128)S(1)} %get-tuple-element.4.b_ref, f32[17,17]{1,0:T(8,128)S(1)} %get-tuple-element.5.g_ref), custom_call_target="tpu_custom_call" | custom-call | tf_op jit(solution)/shard_map/pallas_call | solution.py:460
